TPU v7x, 32 devices: a whole 2x2x4 slice. The times are simulated.
32 devices in a mesh: grp: 2 (over y), seq: 8 (over z, x), head: 2 (over core).
Axes of the slice: x: 2, y: 2, z: 4, core: 2. Of those that a mesh axis runs over, the one named last changes fastest.
Arguments:
- key_cache: bfloat16 [4, 64, 128, 1024], P('grp', ('seq', 'head')), parts along dimension 0, may hold values from -160 to 160, as said below
- value_cache: bfloat16 [4, 64, 128, 1024], P('grp', ('seq', 'head')), parts along dimension 0, may hold values from -16 to 16, as said below
- query: bfloat16 [4, 4096], P('grp', 'head'), parts along dimension 0, may hold values from -48 to 48, as said below
- lengths: int32 [4], P('grp'), parts along dimension 0, may hold values from 128 to 8192, as said below
- block_map: int32 [4, 64], P('grp'), parts along dimension 0, may hold values from 0 to 63, each once within a row
Outputs:
- attended: bfloat16 [4, 4096], P('grp', 'head'), parts along dimension 0
There are 2 independent parts, one for each index of `grp`. A program takes and returns all parts, laid end to end along the dimension named above; each array names one. Nothing has to cross between parts.
Inputs may be any that keep to these rules, and one draw needn't show every extreme that they name: `lengths`: every length is a multiple of 128; in every draw some request has length 8192. `key_cache`: finite entries, drawn afresh for every request, block, token and channel. `value_cache`: finite entries, drawn afresh for every request, block, token and channel. `query`: finite entries, drawn afresh for every request, head and channel.
All inputs are finite; a program needn't handle non-finite values.
Results may differ from a plain program's by a relative error of at most 0.0055.
Values may be sent and summed in bfloat16 or wider, within the bound.
A program may use at most 64 MiB of HBM per device.

v0:
```python
import functools

import jax
import jax.numpy as jnp
from jax import lax
from jax.experimental import pallas as pl
from jax.experimental.pallas import tpu as pltpu
from jax.sharding import PartitionSpec as P

QH = 32
KVH = 8
HD = 128
BLK = 128
REP = QH // KVH
MESH = pl.DeviceIdType.MESH
NEG = -1e30


def kernel(
    n_seq, n_head,
    lengths_hbm, map_hbm, q_hbm, k_hbm, v_hbm, out_ref,
    lengths, block_map, q_ref, small_sem,
    k_buf, v_buf, q_mate, num_send, stat_send, num_recv, stat_recv,
    kv_sem, q_sem, nsend_sem, nrecv_sem, ssend_sem, srecv_sem,
):
    seq = lax.axis_index("seq")
    head = lax.axis_index("head")
    batch, slots = k_hbm.shape[0], k_hbm.shape[1]
    width = k_hbm.shape[3] // n_head
    groups = width // HD
    rows_b = groups * REP
    rows = batch * rows_b
    tokens = slots * BLK
    me = seq * n_head + head
    n_all = n_seq * n_head
    small = n_all <= 16

    def loop(lo, hi, body):
        if small:
            for i in range(lo, hi):
                body(i)
        else:
            def step(i, carry):
                body(i)
                return carry
            lax.fori_loop(lo, hi, step, 0)

    def peer(step):
        return lax.rem(me + step, n_all)

    def place(device):
        return {"seq": device // n_head, "head": lax.rem(device, n_head)}

    barrier = pltpu.get_barrier_semaphore()

    def greet(step):
        pl.semaphore_signal(barrier, inc=1, device_id=place(peer(step)), device_id_type=MESH)

    loop(1, n_all, greet)
    smalls = [pltpu.make_async_copy(a, b, small_sem.at[i]) for i, (a, b) in enumerate(
        ((q_hbm, q_ref), (lengths_hbm, lengths), (map_hbm, block_map)))]
    for copy in smalls:
        copy.start()

    def load(half, which, b):
        owner = lax.rem(head + half, n_head)
        source, target = ((k_hbm, k_buf), (v_hbm, v_buf))[which]
        lanes = pl.ds(pl.multiple_of(owner * width, width), width)
        return pltpu.make_async_copy(
            source.at[b, :, :, lanes], target.at[half, b], kv_sem.at[half, which, b]
        )

    for half in range(n_head):
        for which in range(2):
            for b in range(batch):
                load(half, which, b).start()

    def live_of(b):
        flags = []
        for j in range(slots):
            here = block_map[b, me * slots + j] * BLK < lengths[b]
            flags.append(jnp.broadcast_to(jnp.where(here, 1.0, 0.0), (rows_b, BLK)))
        return jnp.concatenate(flags, axis=1) > 0.5

    def diagonal(q):
        lifted = q.astype(jnp.float32).reshape(rows, HD)
        wide = jnp.concatenate([lifted] * groups, axis=1)
        row_group = lax.rem(lax.broadcasted_iota(jnp.int32, wide.shape, 0), rows_b) // REP
        lane_group = lax.broadcasted_iota(jnp.int32, wide.shape, 1) // HD
        return jnp.where(row_group == lane_group, wide, 0.0).astype(jnp.bfloat16)

    for copy in smalls:
        copy.wait()
    live = [live_of(b) for b in range(batch)]

    def attend(half, q):
        spread = diagonal(q)
        expos, tops, totals, nums = [], [], [], []
        for b in range(batch):
            load(half, 0, b).wait()
        for b in range(batch):
            keys = k_buf[half, b].reshape(tokens, width)
            scores = lax.dot_general(
                spread[b * rows_b:(b + 1) * rows_b], keys, (((1,), (1,)), ((), ())),
                preferred_element_type=jnp.float32,
            ) * (1.0 / HD**0.5)
            scores = jnp.where(live[b], scores, NEG)
            top = jnp.max(scores, axis=1, keepdims=True)
            expo = jnp.where(live[b], jnp.exp(scores - top), 0.0)
            tops.append(top)
            totals.append(jnp.sum(expo, axis=1, keepdims=True))
            expos.append(expo.astype(jnp.bfloat16))
        for b in range(batch):
            load(half, 1, b).wait()
        for b in range(batch):
            values = v_buf[half, b].reshape(tokens, width)
            full = jnp.dot(expos[b], values, preferred_element_type=jnp.float32)
            row_group = lax.broadcasted_iota(jnp.int32, (rows_b, HD), 0) // REP
            part = jnp.zeros((rows_b, HD), jnp.float32)
            for g in range(groups):
                part = jnp.where(row_group == g, full[:, g * HD:(g + 1) * HD], part)
            nums.append(part)
        column = jnp.concatenate(tops + totals + [jnp.zeros((HD - 2 * rows, 1), jnp.float32)], axis=0)
        record = jnp.transpose(jnp.broadcast_to(column, (HD, HD)))[0:1]
        return jnp.concatenate(nums, axis=0), record

    def copies(device, half, slot_of):
        return (
            pltpu.make_async_remote_copy(
                src_ref=stat_send.at[pl.ds(half, 1)], dst_ref=stat_recv.at[pl.ds(slot_of, 1)],
                send_sem=ssend_sem.at[device], recv_sem=srecv_sem.at[slot_of],
                device_id=place(device), device_id_type=MESH,
            ),
            pltpu.make_async_remote_copy(
                src_ref=num_send.at[half], dst_ref=num_recv.at[slot_of],
                send_sem=nsend_sem.at[device], recv_sem=nrecv_sem.at[slot_of],
                device_id=place(device), device_id_type=MESH,
            ),
        )

    def send_half(half):
        def one(d):
            target_seq = lax.rem(seq + d, n_seq)
            target = target_seq * n_head + lax.rem(head + half, n_head)
            for copy in copies(target, half, me):
                copy.start()
        loop(0 if half else 1, n_seq, one)

    pl.semaphore_wait(barrier, n_all - 1)
    q_copy = pltpu.make_async_remote_copy(
        src_ref=q_ref, dst_ref=q_mate, send_sem=q_sem.at[0], recv_sem=q_sem.at[1],
        device_id={"head": lax.rem(head + 1, n_head)}, device_id_type=MESH,
    )
    q_copy.start()
    own_num, own_stat = attend(0, q_ref[...])
    num_send[0] = own_num.astype(jnp.bfloat16)
    stat_send[0:1] = own_stat
    send_half(0)
    q_copy.wait()
    mate_num, mate_stat = attend(1, q_mate[...])
    num_send[1] = mate_num.astype(jnp.bfloat16)
    stat_send[1:2] = mate_stat
    send_half(1)

    stat_recv[pl.ds(me, 1)] = own_stat
    num_recv[me] = own_num.astype(jnp.bfloat16)

    def arrive_stat(step):
        copies(peer(step), 0, peer(step))[0].wait_recv()

    def arrive_num(step):
        copies(peer(step), 0, peer(step))[1].wait_recv()

    loop(1, n_all, arrive_stat)
    stats = stat_recv[...]
    top = stats[:, :rows]
    total = stats[:, rows:2 * rows]
    factor = jnp.exp(top - jnp.max(top, axis=0, keepdims=True))
    share = factor / jnp.sum(factor * total, axis=0, keepdims=True)
    share_columns = jnp.transpose(jnp.concatenate(
        [share, jnp.zeros((n_all, HD - rows), jnp.float32)], axis=1))[:rows]
    loop(1, n_all, arrive_num)
    result = jnp.zeros((rows, HD), jnp.float32)
    for s in range(n_all):
        result = result + share_columns[:, s:s + 1] * num_recv[s].astype(jnp.float32)
    out_ref[...] = result.reshape(batch, rows_b * HD).astype(out_ref.dtype)

    def sent(step):
        for copy in copies(peer(step), 0, me):
            copy.wait_send()

    loop(1, n_all, sent)


def solution(mesh):
    n_seq, n_head = mesh.shape["seq"], mesh.shape["head"]
    n_all = n_seq * n_head

    def on_device(key_cache, value_cache, query, lengths, block_map):
        batch, slots, _, channels = key_cache.shape
        width = channels // n_head
        rows = batch * (width // HD) * REP
        dma = pltpu.SemaphoreType.DMA
        result = pl.pallas_call(
            functools.partial(kernel, n_seq, n_head),
            out_shape=pltpu.VMEM(query.shape, jnp.bfloat16),
            in_specs=[
                *[pl.BlockSpec(memory_space=pl.ANY)] * 5,
            ],
            out_specs=pl.BlockSpec(memory_space=pltpu.VMEM),
            scratch_shapes=[
                pltpu.SMEM(lengths.shape, jnp.int32),
                pltpu.SMEM(block_map.shape, jnp.int32),
                pltpu.VMEM(query.shape, jnp.bfloat16),
                dma((3,)),
                pltpu.VMEM((n_head, batch, slots, BLK, width), jnp.bfloat16),
                pltpu.VMEM((n_head, batch, slots, BLK, width), jnp.bfloat16),
                pltpu.VMEM(query.shape, jnp.bfloat16),
                pltpu.VMEM((n_head, rows, HD), jnp.bfloat16),
                pltpu.VMEM((n_head, HD), jnp.float32),
                pltpu.VMEM((n_all, rows, HD), jnp.bfloat16),
                pltpu.VMEM((n_all, HD), jnp.float32),
                dma((n_head, 2, batch)),
                dma((2,)),
                dma((n_all,)),
                dma((n_all,)),
                dma((n_all,)),
                dma((n_all,)),
            ],
            compiler_params=pltpu.CompilerParams(collective_id=0, has_side_effects=True),
        )(lengths, block_map, query, key_cache, value_cache)
        return result

    placed = (
        P("grp", ("seq", "head"), None, None),
        P("grp", ("seq", "head"), None, None),
        P("grp", "head"),
        P("grp"),
        P("grp", None),
    )
    return jax.shard_map(
        on_device, mesh=mesh, in_specs=placed, out_specs=P("grp", "head"), check_vma=False
    )
```

profile of v0, /device:TPU:0, one launch (start us, length us, event | category | flops | bytes accessed | tf_op | source)
XLA Modules:
  0.0 12.2 jit_solution(6978606552698545273)
XLA Ops:
  0.0 11.6 %shard_map.55 = bf16[2,2048]{1,0:T(2,128)(2,1)S(1)} custom-call(s32[2]{0:T(128)} %lengths_hbm.1, s32[2,64]{1,0:T(2,128)} %map_hbm.1, bf16[2,2048]{1,0:T(2,128)(2,1)} %q_hbm.1, bf16[2,4,128,1024]{3,2,1,0:T(8,128)(2,1)} %k_hbm.1, bf16[2,4,128,1024]{3,2,1,0:T(8,128)(2,1)} %v_hbm.1), custom_call_target="tpu_custom_call" | custom-call | tf_op jit(solution)/shard_map/pallas_call | solution.py:204
  11.6 0.6 %copy.7 = bf16[2,2048]{1,0:T(2,128)(2,1)} copy(bf16[2,2048]{1,0:T(2,128)(2,1)S(1)} %shard_map.55) | data formatting | bytes 16384
where the time goes:
time: 12.3 us; the launch traced here: 12.2 us
  Pallas kernels  11.6 us (94%)
  local copies, waits for them, and re-layouts  0.6 us (5%)
    pallas_call x1, Pallas kernels, on_device(): pl.pallas_call(functools.partial(kernel, n_seq, n_head), out_shape=pltpu....  11.6 us
    unnamed x1, local copies, waits for them, and re-layouts  0.6 us

commit v1 on v0

v1 whole, which is shorter than its diff:
```python
import functools

import jax
import jax.numpy as jnp
from jax import lax
from jax.experimental import pallas as pl
from jax.experimental.pallas import tpu as pltpu
from jax.sharding import PartitionSpec as P

QH = 32
KVH = 8
HD = 128
BLK = 128
REP = QH // KVH
MESH = pl.DeviceIdType.MESH
NEG = -1e30
LOG2E = 1.4426950408889634


def kernel(
    n_seq, n_head,
    lengths_hbm, map_hbm, q_hbm, k_hbm, v_hbm, out_ref,
    lengths, block_map, q_ref, small_sem,
    k_buf, v_buf, q_mate, num_send, stat_send, num_recv, stat_recv, share_ref, order_ref,
    kv_sem, q_sem, nsend_sem, nrecv_sem, ssend_sem, srecv_sem, ready_sem,
):
    seq = lax.axis_index("seq")
    head = lax.axis_index("head")
    batch, slots = k_hbm.shape[0], k_hbm.shape[1]
    width = k_hbm.shape[3] // n_head
    groups = width // HD
    rows_b = groups * REP
    rows = batch * rows_b
    tokens = slots * BLK
    me = seq * n_head + head
    mate = n_head - 1 - head
    n_all = n_seq * n_head
    small = n_all <= 16

    def loop(lo, hi, body):
        if small:
            for i in range(lo, hi):
                body(i)
        else:
            def step(i, carry):
                body(i)
                return carry
            lax.fori_loop(lo, hi, step, 0)

    def turned(d):
        there = seq + d
        return jnp.where(there >= n_seq, there - n_seq, there)

    smalls = [pltpu.make_async_copy(a, b, small_sem.at[i]) for i, (a, b) in enumerate(
        ((lengths_hbm, lengths), (map_hbm, block_map), (q_hbm, q_ref)))]

    def load(half, which):
        owner = jnp.where(half == 0, head, mate)
        source, target = ((k_hbm, k_buf), (v_hbm, v_buf))[which]
        lanes = pl.ds(pl.multiple_of(owner * width, width), width)
        return pltpu.make_async_copy(
            source.at[:, :, :, lanes], target.at[half], kv_sem.at[half, which]
        )

    for copy in smalls:
        copy.start()
    load(0, 0).start()
    for half, which in ((1, 0), (0, 1)):
        load(half, which).start(priority=1)

    barrier = pltpu.get_barrier_semaphore()
    lead = head == n_head - 1

    def q_copy():
        return pltpu.make_async_remote_copy(
            src_ref=q_ref, dst_ref=q_mate, send_sem=q_sem.at[0], recv_sem=q_sem.at[1],
            device_id={"head": mate}, device_id_type=MESH,
        )

    def tell_mate():
        pl.semaphore_signal(ready_sem, inc=1, device_id={"head": mate}, device_id_type=MESH)

    @pl.when(lead)
    def _():
        pl.semaphore_signal(barrier, inc=1, device_id={"head": mate}, device_id_type=MESH)
        pl.semaphore_wait(ready_sem, 1)

        def greet(d):
            pl.semaphore_signal(barrier, inc=1, device_id={"seq": turned(d)}, device_id_type=MESH)

        loop(1, n_seq, greet)

    @pl.when(jnp.logical_not(lead))
    def _():
        pl.semaphore_wait(barrier, 1)
        tell_mate()

    smalls[2].wait()
    q_copy().start()

    def everyone_in():
        @pl.when(lead)
        def _():
            pl.semaphore_wait(barrier, n_seq - 1)
            tell_mate()

        @pl.when(jnp.logical_not(lead))
        def _():
            pl.semaphore_wait(ready_sem, 1)

    def bias_of(b):
        parts = []
        for j in range(slots):
            here = block_map[b, me * slots + j] * BLK < lengths[b]
            parts.append(jnp.broadcast_to(jnp.where(here, 0.0, NEG), (rows_b, BLK)))
        return jnp.concatenate(parts, axis=1)

    def diagonal(q):
        lifted = q.astype(jnp.float32).reshape(rows, HD)
        wide = jnp.concatenate([lifted] * groups, axis=1)
        row_group = lax.rem(lax.broadcasted_iota(jnp.int32, wide.shape, 0), rows_b) // REP
        lane_group = lax.broadcasted_iota(jnp.int32, wide.shape, 1) // HD
        return jnp.where(row_group == lane_group, wide, 0.0).astype(jnp.bfloat16)

    for copy in smalls[:2]:
        copy.wait()
    load(1, 1).start(priority=1)
    bias = [bias_of(b) for b in range(batch)]

    def copies(half, d):
        where = {"seq": turned(d), "head": mate if half else head}
        return (
            pltpu.make_async_remote_copy(
                src_ref=stat_send.at[pl.ds(half, 1)], dst_ref=stat_recv.at[pl.ds(me, 1)],
                send_sem=ssend_sem, recv_sem=srecv_sem, device_id=where, device_id_type=MESH,
            ),
            pltpu.make_async_remote_copy(
                src_ref=num_send.at[half], dst_ref=num_recv.at[me],
                send_sem=nsend_sem, recv_sem=nrecv_sem, device_id=where, device_id_type=MESH,
            ),
        )

    def send(half, which):
        loop(1, n_seq, lambda d: copies(half, d)[which].start())
        if half:
            copies(half, 0)[which].start()

    def score(half, spread):
        load(half, 0).wait()
        return [lax.dot_general(
            spread[b * rows_b:(b + 1) * rows_b], k_buf[half, b].reshape(tokens, width),
            (((1,), (1,)), ((), ())), preferred_element_type=jnp.float32,
        ) for b in range(batch)]

    def soften(half, raw):
        expos, tops, totals = [], [], []
        for b in range(batch):
            scores = raw[b] * (LOG2E / HD**0.5) + bias[b]
            top = jnp.max(scores, axis=1, keepdims=True)
            expo = jnp.exp2(scores - top)
            tops.append(top)
            totals.append(jnp.sum(expo, axis=1, keepdims=True))
            expos.append(expo.astype(jnp.bfloat16))
        column = jnp.concatenate(tops + totals + [jnp.zeros((HD - 2 * rows, 1), jnp.float32)], axis=0)
        stat_send[half:half + 1] = jnp.transpose(jnp.broadcast_to(column, (HD, HD)))[0:1]
        return expos

    def weigh(half, expos):
        load(half, 1).wait()
        row_group = lax.broadcasted_iota(jnp.int32, (rows_b, HD), 0) // REP
        nums = []
        for b in range(batch):
            values = v_buf[half, b].reshape(tokens, width)
            full = jnp.dot(expos[b], values, preferred_element_type=jnp.float32)
            part = jnp.zeros((rows_b, HD), jnp.float32)
            for g in range(groups):
                part = jnp.where(row_group == g, full[:, g * HD:(g + 1) * HD], part)
            nums.append(part)
        num_send[half] = jnp.concatenate(nums, axis=0).astype(jnp.bfloat16)
        send(half, 1)

    raw_own = score(0, diagonal(q_ref[...]))
    q_copy().wait()
    raw_mate = score(1, diagonal(q_mate[...]))
    expos = soften(0, raw_own)
    everyone_in()
    send(0, 0)
    weigh(0, expos)
    expos = soften(1, raw_mate)
    send(1, 0)
    weigh(1, expos)

    all_nums = pltpu.make_async_remote_copy(
        src_ref=num_recv.at[pl.ds(0, n_all - 1)], dst_ref=num_recv.at[pl.ds(0, n_all - 1)],
        send_sem=nsend_sem, recv_sem=nrecv_sem, device_id={"head": mate}, device_id_type=MESH,
    )
    all_stats = pltpu.make_async_remote_copy(
        src_ref=stat_recv.at[pl.ds(0, n_all - 1)], dst_ref=stat_recv.at[pl.ds(0, n_all - 1)],
        send_sem=ssend_sem, recv_sem=srecv_sem, device_id={"head": mate}, device_id_type=MESH,
    )
    all_stats.wait_send()
    all_nums.wait_send()
    stat_recv[pl.ds(me, 1)] = stat_send[0:1]
    num_recv[me] = num_send[0]
    all_stats.wait_recv()
    stats = stat_recv[...]
    top = stats[:, :rows]
    total = stats[:, rows:2 * rows]
    factor = jnp.exp2(top - jnp.max(top, axis=0, keepdims=True))
    share = factor / jnp.sum(factor * total, axis=0, keepdims=True)
    share_columns = jnp.transpose(jnp.concatenate(
        [share, jnp.zeros((n_all, HD - rows), jnp.float32)], axis=1))[:rows]
    for s in range(n_all):
        share_ref[s] = jnp.broadcast_to(share_columns[:, s:s + 1], (rows, HD))
    all_nums.wait_recv()

    def term(s):
        return share_ref[s] * num_recv[s].astype(jnp.float32)

    if small:
        terms = [term(s) for s in range(n_all)]
        while len(terms) > 1:
            terms = [a + b for a, b in zip(terms[::2], terms[1::2])] + terms[len(terms) // 2 * 2:]
        result = terms[0]
    else:
        result = lax.fori_loop(0, n_all, lambda s, acc: acc + term(s), jnp.zeros((rows, HD), jnp.float32))
    for b in range(batch):
        order_ref[pl.ds(b, rows_b, stride=batch), :] = result[b * rows_b:(b + 1) * rows_b]
    out_ref[...] = order_ref[...].astype(out_ref.dtype)


def solution(mesh):
    n_seq, n_head = mesh.shape["seq"], mesh.shape["head"]
    n_all = n_seq * n_head

    def on_device(key_cache, value_cache, query, lengths, block_map):
        batch, slots, _, channels = key_cache.shape
        width = channels // n_head
        rows_b = (width // HD) * REP
        rows = batch * rows_b
        dma = pltpu.SemaphoreType.DMA
        result = pl.pallas_call(
            functools.partial(kernel, n_seq, n_head),
            out_shape=pltpu.VMEM((rows, HD), jnp.bfloat16),
            in_specs=[
                *[pl.BlockSpec(memory_space=pl.ANY)] * 5,
            ],
            out_specs=pl.BlockSpec(memory_space=pltpu.VMEM),
            scratch_shapes=[
                pltpu.SMEM(lengths.shape, jnp.int32),
                pltpu.SMEM(block_map.shape, jnp.int32),
                pltpu.VMEM(query.shape, jnp.bfloat16),
                dma((3,)),
                pltpu.VMEM((n_head, batch, slots, BLK, width), jnp.bfloat16),
                pltpu.VMEM((n_head, batch, slots, BLK, width), jnp.bfloat16),
                pltpu.VMEM(query.shape, jnp.bfloat16),
                pltpu.VMEM((n_head, rows, HD), jnp.bfloat16),
                pltpu.VMEM((n_head, HD), jnp.float32),
                pltpu.VMEM((n_all, rows, HD), jnp.bfloat16),
                pltpu.VMEM((n_all, HD), jnp.float32),
                pltpu.VMEM((n_all, rows, HD), jnp.float32),
                pltpu.VMEM((rows, HD), jnp.float32),
                dma((n_head, 2)),
                dma((2,)),
                dma(()),
                dma(()),
                dma(()),
                dma(()),
                pltpu.SemaphoreType.REGULAR,
            ],
            compiler_params=pltpu.CompilerParams(collective_id=0, has_side_effects=True),
        )(lengths, block_map, query, key_cache, value_cache)
        return result.reshape(rows_b, batch, HD).transpose(1, 0, 2).reshape(batch, rows_b * HD)

    placed = (
        P("grp", ("seq", "head"), None, None),
        P("grp", ("seq", "head"), None, None),
        P("grp", "head"),
        P("grp"),
        P("grp", None),
    )
    return jax.shard_map(
        on_device, mesh=mesh, in_specs=placed, out_specs=P("grp", "head"), check_vma=False
    )
```

time: 12.3 us -> 11.9 us (0.967)
  the two profiles are of different devices: /device:TPU:0 before, /device:TPU:1 now
where the time goes in v1:
time: 11.9 us; the launch traced here: 11.8 us
  Pallas kernels  11.2 us (94%)
  local copies, waits for them, and re-layouts  0.6 us (5%)
    pallas_call x1, Pallas kernels, on_device(): pl.pallas_call(functools.partial(kernel, n_seq, n_head), out_shape=pltpu....  11.2 us
    unnamed x1, local copies, waits for them, and re-layouts  0.6 us

profile of v1, /device:TPU:1, one launch (start us, length us, event | category | flops | bytes accessed | tf_op | source)
XLA Modules:
  0.0 11.8 jit_solution(17717535513274144867)
XLA Ops:
  0.0 11.2 %shard_map.55 = bf16[32,128]{1,0:T(8,128)(2,1)S(1)} custom-call(s32[2]{0:T(128)} %lengths_hbm.1, s32[2,64]{1,0:T(2,128)} %map_hbm.1, bf16[2,2048]{1,0:T(2,128)(2,1)} %q_hbm.1, bf16[2,4,128,1024]{3,2,1,0:T(8,128)(2,1)} %k_hbm.1, bf16[2,4,128,1024]{3,2,1,0:T(8,128)(2,1)} %v_hbm.1), custom_call_target="tpu_custom_call" | custom-call | tf_op jit(solution)/shard_map/pallas_call | solution.py:242
  11.2 0.6 %copy.8 = bf16[2,2048]{1,0:T(2,128)(2,1)} copy(bf16[2,2048]{1,0:T(2,128)(2,1)S(1)} %bitcast.5) | data formatting | bytes 16384

commit v2 on v1

--- a/solution.py
+++ b/solution.py
@@ -11,6 +11,7 @@
 KVH = 8
 HD = 128
 BLK = 128
+TILE = 256
 REP = QH // KVH
 MESH = pl.DeviceIdType.MESH
 NEG = -1e30
@@ -18,7 +19,7 @@
 
 
 def kernel(
-    n_seq, n_head,
+    n_seq, n_head, score_acc, value_acc,
     lengths_hbm, map_hbm, q_hbm, k_hbm, v_hbm, out_ref,
     lengths, block_map, q_ref, small_sem,
     k_buf, v_buf, q_mate, num_send, stat_send, num_recv, stat_recv, share_ref, order_ref,
@@ -32,6 +33,9 @@
     rows_b = groups * REP
     rows = batch * rows_b
     tokens = slots * BLK
+    per = TILE // BLK
+    pieces = tokens // TILE
+    strips = width // TILE
     me = seq * n_head + head
     mate = n_head - 1 - head
     n_all = n_seq * n_head
@@ -48,25 +52,34 @@
             lax.fori_loop(lo, hi, step, 0)
 
     def turned(d):
+        if small and n_seq & (n_seq - 1) == 0:
+            there = seq
+            for bit in range(n_seq.bit_length() - 1):
+                if d >> bit & 1:
+                    there = there + (1 << bit) * (1 - 2 * (seq // (1 << bit) % 2))
+            return there
         there = seq + d
         return jnp.where(there >= n_seq, there - n_seq, there)
 
     smalls = [pltpu.make_async_copy(a, b, small_sem.at[i]) for i, (a, b) in enumerate(
         ((lengths_hbm, lengths), (map_hbm, block_map), (q_hbm, q_ref)))]
 
-    def load(half, which):
+    def load(half, which, piece):
         owner = jnp.where(half == 0, head, mate)
         source, target = ((k_hbm, k_buf), (v_hbm, v_buf))[which]
         lanes = pl.ds(pl.multiple_of(owner * width, width), width)
+        blocks = pl.ds(0, slots) if piece is None else pl.ds(piece * per, per)
         return pltpu.make_async_copy(
-            source.at[:, :, :, lanes], target.at[half], kv_sem.at[half, which]
+            source.at[:, blocks, :, lanes], target.at[half, :, blocks],
+            kv_sem.at[half * 2 + which if piece is None else 2 * n_head + piece],
         )
 
     for copy in smalls:
         copy.start()
-    load(0, 0).start()
-    for half, which in ((1, 0), (0, 1)):
-        load(half, which).start(priority=1)
+    for piece in range(pieces):
+        load(0, 0, piece).start()
+    load(1, 0, None).start(priority=1)
+    load(0, 1, None).start(priority=1)
 
     barrier = pltpu.get_barrier_semaphore()
     lead = head == n_head - 1
@@ -124,7 +137,7 @@
 
     for copy in smalls[:2]:
         copy.wait()
-    load(1, 1).start(priority=1)
+    load(1, 1, None).start(priority=1)
     bias = [bias_of(b) for b in range(batch)]
 
     def copies(half, d):
@@ -140,22 +153,37 @@
             ),
         )
 
-    def send(half, which):
-        loop(1, n_seq, lambda d: copies(half, d)[which].start())
-        if half:
-            copies(half, 0)[which].start()
-
-    def score(half, spread):
-        load(half, 0).wait()
-        return [lax.dot_general(
-            spread[b * rows_b:(b + 1) * rows_b], k_buf[half, b].reshape(tokens, width),
-            (((1,), (1,)), ((), ())), preferred_element_type=jnp.float32,
-        ) for b in range(batch)]
-
-    def soften(half, raw):
+    def send(half, which, turns):
+        if isinstance(turns, list):
+            for d in turns:
+                copies(half, d)[which].start()
+        else:
+            loop(*turns, lambda d: copies(half, d)[which].start())
+
+    row_group = lax.broadcasted_iota(jnp.int32, (rows_b, HD), 0) // REP
+
+    def multiply(acc, b, lhs, rhs, transpose):
+        register = turn[b % 2]
+        turn[b % 2] = 1 - register
+        pltpu.matmul_push_rhs(rhs, register, b % 2, transpose=transpose)
+        pltpu.matmul_acc_lhs(acc, lhs, load_staged_rhs=register)
+
+    turn = [0, 0]
+
+    def score(half, spread, t):
+        for c in range(strips):
+            for b in range(batch):
+                keys = k_buf[half, b, t * per:(t + 1) * per, :, c * TILE:(c + 1) * TILE]
+                multiply(
+                    score_acc[half][b][t], b, spread[b * rows_b:(b + 1) * rows_b, c * TILE:(c + 1) * TILE],
+                    keys.reshape(TILE, TILE), True,
+                )
+
+    def soften(half):
         expos, tops, totals = [], [], []
         for b in range(batch):
-            scores = raw[b] * (LOG2E / HD**0.5) + bias[b]
+            raw = jnp.concatenate([pltpu.matmul_pop(acc) for acc in score_acc[half][b]], axis=1)
+            scores = raw * (LOG2E / HD**0.5) + bias[b]
             top = jnp.max(scores, axis=1, keepdims=True)
             expo = jnp.exp2(scores - top)
             tops.append(top)
@@ -166,29 +194,51 @@
         return expos
 
     def weigh(half, expos):
-        load(half, 1).wait()
-        row_group = lax.broadcasted_iota(jnp.int32, (rows_b, HD), 0) // REP
+        for t in range(pieces):
+            for c in range(strips):
+                for b in range(batch):
+                    values = v_buf[half, b, t * per:(t + 1) * per, :, c * TILE:(c + 1) * TILE]
+                    multiply(
+                        value_acc[half][b][c], b, expos[b][:, t * TILE:(t + 1) * TILE],
+                        values.reshape(TILE, TILE), False,
+                    )
+
+    def finish(half):
         nums = []
         for b in range(batch):
-            values = v_buf[half, b].reshape(tokens, width)
-            full = jnp.dot(expos[b], values, preferred_element_type=jnp.float32)
             part = jnp.zeros((rows_b, HD), jnp.float32)
-            for g in range(groups):
-                part = jnp.where(row_group == g, full[:, g * HD:(g + 1) * HD], part)
+            for c in range(strips):
+                full = pltpu.matmul_pop(value_acc[half][b][c])
+                for g in range(TILE // HD):
+                    part = jnp.where(row_group == c * (TILE // HD) + g, full[:, g * HD:(g + 1) * HD], part)
             nums.append(part)
         num_send[half] = jnp.concatenate(nums, axis=0).astype(jnp.bfloat16)
-        send(half, 1)
-
-    raw_own = score(0, diagonal(q_ref[...]))
+
+    own_turns, mate_turns = (1, n_seq), (0, n_seq)
+    if small:
+        own_turns, mate_turns = list(range(n_seq - 1, 0, -1)), list(range(n_seq - 1, -1, -1))
+    spread = diagonal(q_ref[...])
+    for t in range(pieces):
+        load(0, 0, t).wait()
+        score(0, spread, t)
     q_copy().wait()
-    raw_mate = score(1, diagonal(q_mate[...]))
-    expos = soften(0, raw_own)
+    spread = diagonal(q_mate[...])
+    load(1, 0, None).wait()
+    for t in range(pieces):
+        score(1, spread, t)
+    expos = soften(0)
     everyone_in()
-    send(0, 0)
+    send(0, 0, own_turns)
+    load(0, 1, None).wait()
     weigh(0, expos)
-    expos = soften(1, raw_mate)
-    send(1, 0)
+    expos = soften(1)
+    send(1, 0, mate_turns)
+    load(1, 1, None).wait()
     weigh(1, expos)
+    finish(0)
+    send(0, 1, own_turns)
+    finish(1)
+    send(1, 1, mate_turns)
 
     all_nums = pltpu.make_async_remote_copy(
         src_ref=num_recv.at[pl.ds(0, n_all - 1)], dst_ref=num_recv.at[pl.ds(0, n_all - 1)],
@@ -229,6 +279,21 @@
     out_ref[...] = order_ref[...].astype(out_ref.dtype)
 
 
+def with_accumulators(n_seq, n_head, *refs):
+    batch, slots = refs[3].shape[0], refs[3].shape[1]
+    width = refs[3].shape[3] // n_head
+    rows_b = width // HD * REP
+
+    def accumulators(count):
+        return [[[pltpu.ACC(b % 2)((rows_b, TILE), jnp.float32) for _ in range(count)]
+                 for b in range(batch)] for _ in range(n_head)]
+
+    pl.run_scoped(
+        lambda score_acc, value_acc: kernel(n_seq, n_head, score_acc, value_acc, *refs),
+        accumulators(slots * BLK // TILE), accumulators(width // TILE),
+    )
+
+
 def solution(mesh):
     n_seq, n_head = mesh.shape["seq"], mesh.shape["head"]
     n_all = n_seq * n_head
@@ -240,7 +305,7 @@
         rows = batch * rows_b
         dma = pltpu.SemaphoreType.DMA
         result = pl.pallas_call(
-            functools.partial(kernel, n_seq, n_head),
+            functools.partial(with_accumulators, n_seq, n_head),
             out_shape=pltpu.VMEM((rows, HD), jnp.bfloat16),
             in_specs=[
                 *[pl.BlockSpec(memory_space=pl.ANY)] * 5,
@@ -260,7 +325,7 @@
                 pltpu.VMEM((n_all, HD), jnp.float32),
                 pltpu.VMEM((n_all, rows, HD), jnp.float32),
                 pltpu.VMEM((rows, HD), jnp.float32),
-                dma((n_head, 2)),
+                dma((2 * n_head + slots * BLK // TILE,)),
                 dma((2,)),
                 dma(()),
                 dma(()),

time: 11.9 us -> 11.6 us (0.975)
  the two profiles are of different devices: /device:TPU:1 before, /device:TPU:0 now
where the time goes in v2:
time: 11.6 us; the launch traced here: 11.5 us
  Pallas kernels  10.8 us (93%)
  local copies, waits for them, and re-layouts  0.6 us (5%)
    pallas_call x1, Pallas kernels, on_device(): pl.pallas_call(functools.partial(with_accumulators, n_seq, n_head), out_s...  10.8 us
    unnamed x1, local copies, waits for them, and re-layouts  0.6 us

profile of v2, /device:TPU:0, one launch (start us, length us, event | category | flops | bytes accessed | tf_op | source)
XLA Modules:
  0.0 11.5 jit_solution(14640993037384135977)
XLA Ops:
  0.0 10.8 %shard_map.55 = bf16[32,128]{1,0:T(8,128)(2,1)S(1)} custom-call(s32[2]{0:T(128)} %refs_0_.1, s32[2,64]{1,0:T(2,128)} %refs_1_.1, bf16[2,2048]{1,0:T(2,128)(2,1)} %refs_2_.1, bf16[2,4,128,1024]{3,2,1,0:T(8,128)(2,1)} %refs_3_.1, bf16[2,4,128,1024]{3,2,1,0:T(8,128)(2,1)} %refs_4_.1), custom_call_target="tpu_custom_call" | custom-call | tf_op jit(solution)/shard_map/pallas_call | solution.py:307
  10.9 0.6 %copy.8 = bf16[2,2048]{1,0:T(2,128)(2,1)} copy(bf16[2,2048]{1,0:T(2,128)(2,1)S(1)} %bitcast.5) | data formatting | bytes 16384

commit v3 on v2

--- a/solution.py
+++ b/solution.py
@@ -52,34 +52,26 @@
             lax.fori_loop(lo, hi, step, 0)
 
     def turned(d):
-        if small and n_seq & (n_seq - 1) == 0:
-            there = seq
-            for bit in range(n_seq.bit_length() - 1):
-                if d >> bit & 1:
-                    there = there + (1 << bit) * (1 - 2 * (seq // (1 << bit) % 2))
-            return there
-        there = seq + d
-        return jnp.where(there >= n_seq, there - n_seq, there)
+        return jnp.where(d == n_seq - 1, seq, d + jnp.where(d >= seq, 1, 0))
 
     smalls = [pltpu.make_async_copy(a, b, small_sem.at[i]) for i, (a, b) in enumerate(
         ((lengths_hbm, lengths), (map_hbm, block_map), (q_hbm, q_ref)))]
 
-    def load(half, which, piece):
+    def load(half, which, piece=None):
         owner = jnp.where(half == 0, head, mate)
         source, target = ((k_hbm, k_buf), (v_hbm, v_buf))[which]
         lanes = pl.ds(pl.multiple_of(owner * width, width), width)
         blocks = pl.ds(0, slots) if piece is None else pl.ds(piece * per, per)
         return pltpu.make_async_copy(
             source.at[:, blocks, :, lanes], target.at[half, :, blocks],
-            kv_sem.at[half * 2 + which if piece is None else 2 * n_head + piece],
+            kv_sem.at[half * (pieces + 1) + (pieces if piece is None else piece)],
         )
 
     for copy in smalls:
         copy.start()
     for piece in range(pieces):
         load(0, 0, piece).start()
-    load(1, 0, None).start(priority=1)
-    load(0, 1, None).start(priority=1)
+    load(0, 1).start(priority=1)
 
     barrier = pltpu.get_barrier_semaphore()
     lead = head == n_head - 1
@@ -101,7 +93,7 @@
         def greet(d):
             pl.semaphore_signal(barrier, inc=1, device_id={"seq": turned(d)}, device_id_type=MESH)
 
-        loop(1, n_seq, greet)
+        loop(0, n_seq - 1, greet)
 
     @pl.when(jnp.logical_not(lead))
     def _():
@@ -137,7 +129,9 @@
 
     for copy in smalls[:2]:
         copy.wait()
-    load(1, 1, None).start(priority=1)
+    for piece in range(pieces):
+        load(1, 0, piece).start()
+    load(1, 1).start(priority=1)
     bias = [bias_of(b) for b in range(batch)]
 
     def copies(half, d):
@@ -154,11 +148,7 @@
         )
 
     def send(half, which, turns):
-        if isinstance(turns, list):
-            for d in turns:
-                copies(half, d)[which].start()
-        else:
-            loop(*turns, lambda d: copies(half, d)[which].start())
+        loop(*turns, lambda d: copies(half, d)[which].start())
 
     row_group = lax.broadcasted_iota(jnp.int32, (rows_b, HD), 0) // REP
 
@@ -214,31 +204,34 @@
             nums.append(part)
         num_send[half] = jnp.concatenate(nums, axis=0).astype(jnp.bfloat16)
 
-    own_turns, mate_turns = (1, n_seq), (0, n_seq)
-    if small:
-        own_turns, mate_turns = list(range(n_seq - 1, 0, -1)), list(range(n_seq - 1, -1, -1))
+    own_turns, mate_turns, first = (0, n_seq - 1), (0, n_seq), max(1, n_seq // 4)
     spread = diagonal(q_ref[...])
     for t in range(pieces):
         load(0, 0, t).wait()
         score(0, spread, t)
-    q_copy().wait()
-    spread = diagonal(q_mate[...])
-    load(1, 0, None).wait()
-    for t in range(pieces):
-        score(1, spread, t)
     expos = soften(0)
     everyone_in()
     send(0, 0, own_turns)
-    load(0, 1, None).wait()
+    load(0, 1).wait()
     weigh(0, expos)
+    q_copy().wait()
+    spread = diagonal(q_mate[...])
+    for t in range(0, 1):
+        load(1, 0, t).wait()
+        score(1, spread, t)
+    finish(0)
+    send(0, 1, (0, first))
+    for t in range(1, pieces):
+        load(1, 0, t).wait()
+        score(1, spread, t)
     expos = soften(1)
     send(1, 0, mate_turns)
-    load(1, 1, None).wait()
+    load(1, 1).wait()
     weigh(1, expos)
-    finish(0)
-    send(0, 1, own_turns)
     finish(1)
-    send(1, 1, mate_turns)
+    send(1, 1, (0, first))
+    send(0, 1, (first, n_seq - 1))
+    send(1, 1, (first, n_seq))
 
     all_nums = pltpu.make_async_remote_copy(
         src_ref=num_recv.at[pl.ds(0, n_all - 1)], dst_ref=num_recv.at[pl.ds(0, n_all - 1)],
@@ -325,7 +318,7 @@
                 pltpu.VMEM((n_all, HD), jnp.float32),
                 pltpu.VMEM((n_all, rows, HD), jnp.float32),
                 pltpu.VMEM((rows, HD), jnp.float32),
-                dma((2 * n_head + slots * BLK // TILE,)),
+                dma((n_head * (slots * BLK // TILE + 1),)),
                 dma((2,)),
                 dma(()),
                 dma(()),

time: 11.6 us -> 10.9 us (0.940)
  Pallas kernels: 10.8 us -> 10.2 us
    pallas_call x1, Pallas kernels: 10.8 us -> 10.2 us  [on_device(): pl.pallas_call(functools.partial(with_accumulators, n_seq, n_head), out_s...]
where the time goes in v3:
time: 10.9 us; the launch traced here: 10.8 us
  Pallas kernels  10.2 us (94%)
  local copies, waits for them, and re-layouts  0.6 us (6%)
    pallas_call x1, Pallas kernels, on_device(): pl.pallas_call(functools.partial(with_accumulators, n_seq, n_head), out_s...  10.2 us
    unnamed x1, local copies, waits for them, and re-layouts  0.6 us

profile of v3, /device:TPU:0, one launch (start us, length us, event | category | flops | bytes accessed | tf_op | source)
XLA Modules:
  0.0 10.8 jit_solution(9204840662506948565)
XLA Ops:
  0.0 10.2 %shard_map.55 = bf16[32,128]{1,0:T(8,128)(2,1)S(1)} custom-call(s32[2]{0:T(128)} %refs_0_.1, s32[2,64]{1,0:T(2,128)} %refs_1_.1, bf16[2,2048]{1,0:T(2,128)(2,1)} %refs_2_.1, bf16[2,4,128,1024]{3,2,1,0:T(8,128)(2,1)} %refs_3_.1, bf16[2,4,128,1024]{3,2,1,0:T(8,128)(2,1)} %refs_4_.1), custom_call_target="tpu_custom_call" | custom-call | tf_op jit(solution)/shard_map/pallas_call | solution.py:300
  10.2 0.6 %copy.8 = bf16[2,2048]{1,0:T(2,128)(2,1)} copy(bf16[2,2048]{1,0:T(2,128)(2,1)S(1)} %bitcast.5) | data formatting | bytes 16384

commit v4 on v3

--- a/solution.py
+++ b/solution.py
@@ -19,11 +19,11 @@
 
 
 def kernel(
-    n_seq, n_head, score_acc, value_acc,
+    n_seq, n_head, score_acc, value_acc, small_sem, kv_sem, qsend_sem, nsend_sem, ssend_sem,
     lengths_hbm, map_hbm, q_hbm, k_hbm, v_hbm, out_ref,
-    lengths, block_map, q_ref, small_sem,
+    lengths, block_map, q_ref,
     k_buf, v_buf, q_mate, num_send, stat_send, num_recv, stat_recv, share_ref, order_ref,
-    kv_sem, q_sem, nsend_sem, nrecv_sem, ssend_sem, srecv_sem, ready_sem,
+    q_sem, nrecv_sem, srecv_sem, ready_sem,
 ):
     seq = lax.axis_index("seq")
     head = lax.axis_index("head")
@@ -78,7 +78,7 @@
 
     def q_copy():
         return pltpu.make_async_remote_copy(
-            src_ref=q_ref, dst_ref=q_mate, send_sem=q_sem.at[0], recv_sem=q_sem.at[1],
+            src_ref=q_ref, dst_ref=q_mate, send_sem=qsend_sem, recv_sem=q_sem,
             device_id={"head": mate}, device_id_type=MESH,
         )
 
@@ -151,6 +151,8 @@
         loop(*turns, lambda d: copies(half, d)[which].start())
 
     row_group = lax.broadcasted_iota(jnp.int32, (rows_b, HD), 0) // REP
+    row = lax.broadcasted_iota(jnp.int32, (rows, HD), 0)
+    lane = lax.broadcasted_iota(jnp.int32, (rows, HD), 1)
 
     def multiply(acc, b, lhs, rhs, transpose):
         register = turn[b % 2]
@@ -179,8 +181,9 @@
             tops.append(top)
             totals.append(jnp.sum(expo, axis=1, keepdims=True))
             expos.append(expo.astype(jnp.bfloat16))
-        column = jnp.concatenate(tops + totals + [jnp.zeros((HD - 2 * rows, 1), jnp.float32)], axis=0)
-        stat_send[half:half + 1] = jnp.transpose(jnp.broadcast_to(column, (HD, HD)))[0:1]
+        record = jnp.where(lane == row, jnp.concatenate(tops, axis=0), 0.0)
+        record = jnp.where(lane == row + rows, jnp.concatenate(totals, axis=0), record)
+        stat_send[half:half + 1] = jnp.sum(record, axis=0, keepdims=True)
         return expos
 
     def weigh(half, expos):
@@ -247,14 +250,16 @@
     num_recv[me] = num_send[0]
     all_stats.wait_recv()
     stats = stat_recv[...]
-    top = stats[:, :rows]
-    total = stats[:, rows:2 * rows]
-    factor = jnp.exp2(top - jnp.max(top, axis=0, keepdims=True))
-    share = factor / jnp.sum(factor * total, axis=0, keepdims=True)
-    share_columns = jnp.transpose(jnp.concatenate(
-        [share, jnp.zeros((n_all, HD - rows), jnp.float32)], axis=1))[:rows]
+    factor = jnp.exp2(stats - jnp.max(stats, axis=0, keepdims=True))
+
+    def column(line):
+        return jnp.sum(jnp.where(lane == row, line, 0.0), axis=1, keepdims=True)
+
     for s in range(n_all):
-        share_ref[s] = jnp.broadcast_to(share_columns[:, s:s + 1], (rows, HD))
+        share_ref[s] = jnp.broadcast_to(column(factor[s:s + 1]), (rows, HD))
+    whole = jnp.sum(factor[:, :rows] * stats[:, rows:2 * rows], axis=0, keepdims=True)
+    whole = jnp.concatenate([whole, jnp.ones((1, HD - rows), jnp.float32)], axis=1)
+    scale = column(1.0 / whole)
     all_nums.wait_recv()
 
     def term(s):
@@ -267,6 +272,7 @@
         result = terms[0]
     else:
         result = lax.fori_loop(0, n_all, lambda s, acc: acc + term(s), jnp.zeros((rows, HD), jnp.float32))
+    result = result * scale
     for b in range(batch):
         order_ref[pl.ds(b, rows_b, stride=batch), :] = result[b * rows_b:(b + 1) * rows_b]
     out_ref[...] = order_ref[...].astype(out_ref.dtype)
@@ -276,14 +282,16 @@
     batch, slots = refs[3].shape[0], refs[3].shape[1]
     width = refs[3].shape[3] // n_head
     rows_b = width // HD * REP
+    dma = pltpu.SemaphoreType.DMA
 
     def accumulators(count):
         return [[[pltpu.ACC(b % 2)((rows_b, TILE), jnp.float32) for _ in range(count)]
                  for b in range(batch)] for _ in range(n_head)]
 
     pl.run_scoped(
-        lambda score_acc, value_acc: kernel(n_seq, n_head, score_acc, value_acc, *refs),
+        lambda *scoped: kernel(n_seq, n_head, *scoped, *refs),
         accumulators(slots * BLK // TILE), accumulators(width // TILE),
+        dma((3,)), dma((n_head * (slots * BLK // TILE + 1),)), dma(()), dma(()), dma(()),
     )
 
 
@@ -308,7 +316,6 @@
                 pltpu.SMEM(lengths.shape, jnp.int32),
                 pltpu.SMEM(block_map.shape, jnp.int32),
                 pltpu.VMEM(query.shape, jnp.bfloat16),
-                dma((3,)),
                 pltpu.VMEM((n_head, batch, slots, BLK, width), jnp.bfloat16),
                 pltpu.VMEM((n_head, batch, slots, BLK, width), jnp.bfloat16),
                 pltpu.VMEM(query.shape, jnp.bfloat16),
@@ -318,9 +325,6 @@
                 pltpu.VMEM((n_all, HD), jnp.float32),
                 pltpu.VMEM((n_all, rows, HD), jnp.float32),
                 pltpu.VMEM((rows, HD), jnp.float32),
-                dma((n_head * (slots * BLK // TILE + 1),)),
-                dma((2,)),
-                dma(()),
                 dma(()),
                 dma(()),
                 dma(()),

time: 10.9 us -> 10.7 us (0.982)
  Pallas kernels: 10.2 us -> 9.9 us
    pallas_call x1, Pallas kernels: 10.2 us -> 9.9 us  [on_device(): pl.pallas_call(functools.partial(with_accumulators, n_seq, n_head), out_s...]
where the time goes in v4:
time: 10.7 us; the launch traced here: 10.5 us
  Pallas kernels  9.9 us (93%)
  local copies, waits for them, and re-layouts  0.6 us (6%)
    pallas_call x1, Pallas kernels, on_device(): pl.pallas_call(functools.partial(with_accumulators, n_seq, n_head), out_s...  9.9 us
    unnamed x1, local copies, waits for them, and re-layouts  0.6 us

profile of v4, /device:TPU:0, one launch (start us, length us, event | category | flops | bytes accessed | tf_op | source)
XLA Modules:
  0.0 10.5 jit_solution(8324577004051388921)
XLA Ops:
  0.0 9.9 %shard_map.55 = bf16[32,128]{1,0:T(8,128)(2,1)S(1)} custom-call(s32[2]{0:T(128)} %refs_0_.1, s32[2,64]{1,0:T(2,128)} %refs_1_.1, bf16[2,2048]{1,0:T(2,128)(2,1)} %refs_2_.1, bf16[2,4,128,1024]{3,2,1,0:T(8,128)(2,1)} %refs_3_.1, bf16[2,4,128,1024]{3,2,1,0:T(8,128)(2,1)} %refs_4_.1), custom_call_target="tpu_custom_call" | custom-call | tf_op jit(solution)/shard_map/pallas_call | solution.py:308
  9.9 0.6 %copy.8 = bf16[2,2048]{1,0:T(2,128)(2,1)} copy(bf16[2,2048]{1,0:T(2,128)(2,1)S(1)} %bitcast.5) | data formatting | bytes 16384

commit v5 on v4

--- a/solution.py
+++ b/solution.py
@@ -172,21 +172,22 @@
                 )
 
     def soften(half):
-        expos, tops, totals = [], [], []
+        soft = []
         for b in range(batch):
             raw = jnp.concatenate([pltpu.matmul_pop(acc) for acc in score_acc[half][b]], axis=1)
             scores = raw * (LOG2E / HD**0.5) + bias[b]
             top = jnp.max(scores, axis=1, keepdims=True)
-            expo = jnp.exp2(scores - top)
-            tops.append(top)
-            totals.append(jnp.sum(expo, axis=1, keepdims=True))
-            expos.append(expo.astype(jnp.bfloat16))
-        record = jnp.where(lane == row, jnp.concatenate(tops, axis=0), 0.0)
+            soft.append((jnp.exp2(scores - top), top))
+        return soft
+
+    def note(half, soft):
+        totals = [jnp.sum(expo, axis=1, keepdims=True) for expo, _ in soft]
+        record = jnp.where(lane == row, jnp.concatenate([top for _, top in soft], axis=0), 0.0)
         record = jnp.where(lane == row + rows, jnp.concatenate(totals, axis=0), record)
         stat_send[half:half + 1] = jnp.sum(record, axis=0, keepdims=True)
-        return expos
-
-    def weigh(half, expos):
+
+    def weigh(half, soft):
+        expos = [expo.astype(jnp.bfloat16) for expo, _ in soft]
         for t in range(pieces):
             for c in range(strips):
                 for b in range(batch):
@@ -212,27 +213,30 @@
     for t in range(pieces):
         load(0, 0, t).wait()
         score(0, spread, t)
-    expos = soften(0)
+    soft = soften(0)
+    load(0, 1).wait()
+    weigh(0, soft)
+    note(0, soft)
     everyone_in()
-    send(0, 0, own_turns)
-    load(0, 1).wait()
-    weigh(0, expos)
+    send(0, 0, (0, first))
     q_copy().wait()
     spread = diagonal(q_mate[...])
-    for t in range(0, 1):
-        load(1, 0, t).wait()
-        score(1, spread, t)
+    load(1, 0, 0).wait()
+    score(1, spread, 0)
     finish(0)
     send(0, 1, (0, first))
     for t in range(1, pieces):
         load(1, 0, t).wait()
         score(1, spread, t)
-    expos = soften(1)
-    send(1, 0, mate_turns)
+    soft = soften(1)
     load(1, 1).wait()
-    weigh(1, expos)
+    weigh(1, soft)
+    note(1, soft)
+    send(1, 0, (0, first))
     finish(1)
     send(1, 1, (0, first))
+    send(0, 0, (first, n_seq - 1))
+    send(1, 0, (first, n_seq))
     send(0, 1, (first, n_seq - 1))
     send(1, 1, (first, n_seq))
 

time: 10.7 us -> 10.5 us (0.981)
  Pallas kernels: 9.9 us -> 9.77 us
    pallas_call x1, Pallas kernels: 9.9 us -> 9.77 us  [on_device(): pl.pallas_call(functools.partial(with_accumulators, n_seq, n_head), out_s...]
where the time goes in v5:
time: 10.5 us; the launch traced here: 10.4 us
  Pallas kernels  9.77 us (93%)
  local copies, waits for them, and re-layouts  0.6 us (6%)
    pallas_call x1, Pallas kernels, on_device(): pl.pallas_call(functools.partial(with_accumulators, n_seq, n_head), out_s...  9.77 us
    unnamed x1, local copies, waits for them, and re-layouts  0.6 us

profile of v5, /device:TPU:0, one launch (start us, length us, event | category | flops | bytes accessed | tf_op | source)
XLA Modules:
  0.0 10.4 jit_solution(1468899691916443545)
XLA Ops:
  0.0 9.8 %shard_map.55 = bf16[32,128]{1,0:T(8,128)(2,1)S(1)} custom-call(s32[2]{0:T(128)} %refs_0_.1, s32[2,64]{1,0:T(2,128)} %refs_1_.1, bf16[2,2048]{1,0:T(2,128)(2,1)} %refs_2_.1, bf16[2,4,128,1024]{3,2,1,0:T(8,128)(2,1)} %refs_3_.1, bf16[2,4,128,1024]{3,2,1,0:T(8,128)(2,1)} %refs_4_.1), custom_call_target="tpu_custom_call" | custom-call | tf_op jit(solution)/shard_map/pallas_call | solution.py:312
  9.8 0.6 %copy.8 = bf16[2,2048]{1,0:T(2,128)(2,1)} copy(bf16[2,2048]{1,0:T(2,128)(2,1)S(1)} %bitcast.5) | data formatting | bytes 16384

commit v6 on v5

--- a/solution.py
+++ b/solution.py
@@ -154,31 +154,32 @@
     row = lax.broadcasted_iota(jnp.int32, (rows, HD), 0)
     lane = lax.broadcasted_iota(jnp.int32, (rows, HD), 1)
 
-    def multiply(acc, b, lhs, rhs, transpose):
-        register = turn[b % 2]
-        turn[b % 2] = 1 - register
-        pltpu.matmul_push_rhs(rhs, register, b % 2, transpose=transpose)
-        pltpu.matmul_acc_lhs(acc, lhs, load_staged_rhs=register)
-
-    turn = [0, 0]
+    def push(ref, half, b, i):
+        t, c = i // strips, i % strips
+        tile = ref[half, b, t * per:(t + 1) * per, :, c * TILE:(c + 1) * TILE].reshape(TILE, TILE)
+        pltpu.matmul_push_rhs(tile, i % 2, b % 2, transpose=ref is k_buf)
+
+    def fill(ref, half, lo, hi):
+        for i in range(lo, hi):
+            for b in range(batch):
+                push(ref, half, b, i)
 
     def score(half, spread, t):
-        for c in range(strips):
+        for i in range(t * strips, (t + 1) * strips):
             for b in range(batch):
-                keys = k_buf[half, b, t * per:(t + 1) * per, :, c * TILE:(c + 1) * TILE]
-                multiply(
-                    score_acc[half][b][t], b, spread[b * rows_b:(b + 1) * rows_b, c * TILE:(c + 1) * TILE],
-                    keys.reshape(TILE, TILE), True,
-                )
-
-    def soften(half):
-        soft = []
+                c = i % strips
+                lhs = spread[b * rows_b:(b + 1) * rows_b, c * TILE:(c + 1) * TILE]
+                pltpu.matmul_acc_lhs(score_acc[half][b][t], lhs, load_staged_rhs=i % 2)
+
+    def peak(half):
+        scores = []
         for b in range(batch):
             raw = jnp.concatenate([pltpu.matmul_pop(acc) for acc in score_acc[half][b]], axis=1)
-            scores = raw * (LOG2E / HD**0.5) + bias[b]
-            top = jnp.max(scores, axis=1, keepdims=True)
-            soft.append((jnp.exp2(scores - top), top))
-        return soft
+            scores.append(raw * (LOG2E / HD**0.5) + bias[b])
+        return [(x, jnp.max(x, axis=1, keepdims=True)) for x in scores]
+
+    def soften(peaks):
+        return [(jnp.exp2(x - top), top) for x, top in peaks]
 
     def note(half, soft):
         totals = [jnp.sum(expo, axis=1, keepdims=True) for expo, _ in soft]
@@ -188,14 +189,13 @@
 
     def weigh(half, soft):
         expos = [expo.astype(jnp.bfloat16) for expo, _ in soft]
-        for t in range(pieces):
-            for c in range(strips):
-                for b in range(batch):
-                    values = v_buf[half, b, t * per:(t + 1) * per, :, c * TILE:(c + 1) * TILE]
-                    multiply(
-                        value_acc[half][b][c], b, expos[b][:, t * TILE:(t + 1) * TILE],
-                        values.reshape(TILE, TILE), False,
-                    )
+        for i in range(pieces * strips):
+            t, c = i // strips, i % strips
+            for b in range(batch):
+                pltpu.matmul_acc_lhs(
+                    value_acc[half][b][c], expos[b][:, t * TILE:(t + 1) * TILE], load_staged_rhs=i % 2)
+            if i + 2 < pieces * strips:
+                fill(v_buf, half, i + 2, i + 3)
 
     def finish(half):
         nums = []
@@ -212,24 +212,31 @@
     spread = diagonal(q_ref[...])
     for t in range(pieces):
         load(0, 0, t).wait()
+        fill(k_buf, 0, t * strips, (t + 1) * strips)
         score(0, spread, t)
-    soft = soften(0)
+    peaks = peak(0)
+    soft = soften(peaks)
     load(0, 1).wait()
+    fill(v_buf, 0, 0, 2)
     weigh(0, soft)
     note(0, soft)
     everyone_in()
     send(0, 0, (0, first))
+    finish(0)
+    send(0, 1, (0, first))
+    load(1, 0, 0).wait()
+    fill(k_buf, 1, 0, strips)
     q_copy().wait()
     spread = diagonal(q_mate[...])
-    load(1, 0, 0).wait()
     score(1, spread, 0)
-    finish(0)
-    send(0, 1, (0, first))
     for t in range(1, pieces):
         load(1, 0, t).wait()
+        fill(k_buf, 1, t * strips, (t + 1) * strips)
         score(1, spread, t)
-    soft = soften(1)
+    peaks = peak(1)
+    soft = soften(peaks)
     load(1, 1).wait()
+    fill(v_buf, 1, 0, 2)
     weigh(1, soft)
     note(1, soft)
     send(1, 0, (0, first))

time: 10.5 us -> 10.5 us (level)
  no operation moved by 1% of the time
where the time goes in v6:
time: 10.5 us; the launch traced here: 10.3 us
  Pallas kernels  9.71 us (92%)
  local copies, waits for them, and re-layouts  0.6 us (6%)
    pallas_call x1, Pallas kernels, on_device(): pl.pallas_call(functools.partial(with_accumulators, n_seq, n_head), out_s...  9.71 us
    unnamed x1, local copies, waits for them, and re-layouts  0.6 us

profile of v6, /device:TPU:0, one launch (start us, length us, event | category | flops | bytes accessed | tf_op | source)
XLA Modules:
  0.0 10.3 jit_solution(9741904152978979083)
XLA Ops:
  0.0 9.7 %shard_map.55 = bf16[32,128]{1,0:T(8,128)(2,1)S(1)} custom-call(s32[2]{0:T(128)} %refs_0_.1, s32[2,64]{1,0:T(2,128)} %refs_1_.1, bf16[2,2048]{1,0:T(2,128)(2,1)} %refs_2_.1, bf16[2,4,128,1024]{3,2,1,0:T(8,128)(2,1)} %refs_3_.1, bf16[2,4,128,1024]{3,2,1,0:T(8,128)(2,1)} %refs_4_.1), custom_call_target="tpu_custom_call" | custom-call | tf_op jit(solution)/shard_map/pallas_call | solution.py:319
  9.7 0.6 %copy.8 = bf16[2,2048]{1,0:T(2,128)(2,1)} copy(bf16[2,2048]{1,0:T(2,128)(2,1)S(1)} %bitcast.5) | data formatting | bytes 16384

commit v7 on v5

--- a/solution.py
+++ b/solution.py
@@ -71,7 +71,9 @@
         copy.start()
     for piece in range(pieces):
         load(0, 0, piece).start()
-    load(0, 1).start(priority=1)
+    load(0, 1).start(priority=0)
+    for piece in range(pieces):
+        load(1, 0, piece).start(priority=1)
 
     barrier = pltpu.get_barrier_semaphore()
     lead = head == n_head - 1
@@ -129,8 +131,6 @@
 
     for copy in smalls[:2]:
         copy.wait()
-    for piece in range(pieces):
-        load(1, 0, piece).start()
     load(1, 1).start(priority=1)
     bias = [bias_of(b) for b in range(batch)]
 

time: 10.5 us -> 10.5 us (level)
  no operation moved by 1% of the time
where the time goes in v7:
time: 10.5 us; the launch traced here: 10.4 us
  Pallas kernels  9.78 us (93%)
  local copies, waits for them, and re-layouts  0.6 us (6%)
    pallas_call x1, Pallas kernels, on_device(): pl.pallas_call(functools.partial(with_accumulators, n_seq, n_head), out_s...  9.78 us
    unnamed x1, local copies, waits for them, and re-layouts  0.6 us

profile of v7, /device:TPU:0, one launch (start us, length us, event | category | flops | bytes accessed | tf_op | source)
XLA Modules:
  0.0 10.4 jit_solution(4712042668843670700)
XLA Ops:
  0.0 9.8 %shard_map.55 = bf16[32,128]{1,0:T(8,128)(2,1)S(1)} custom-call(s32[2]{0:T(128)} %refs_0_.1, s32[2,64]{1,0:T(2,128)} %refs_1_.1, bf16[2,2048]{1,0:T(2,128)(2,1)} %refs_2_.1, bf16[2,4,128,1024]{3,2,1,0:T(8,128)(2,1)} %refs_3_.1, bf16[2,4,128,1024]{3,2,1,0:T(8,128)(2,1)} %refs_4_.1), custom_call_target="tpu_custom_call" | custom-call | tf_op jit(solution)/shard_map/pallas_call | solution.py:312
  9.8 0.6 %copy.8 = bf16[2,2048]{1,0:T(2,128)(2,1)} copy(bf16[2,2048]{1,0:T(2,128)(2,1)S(1)} %bitcast.5) | data formatting | bytes 16384
